TPU v7x, 32 devices: a whole 2x2x4 slice. The times are simulated.
32 devices in a mesh: dp: 4 (over z), seq: 8 (over y, x, core).
Axes of the slice: x: 2, y: 2, z: 4, core: 2. Of those that a mesh axis runs over, the one named last changes fastest.
Arguments:
- queries: bfloat16 [4, 2048, 512], P('dp', 'seq'), may hold values from -0.890625 to 0.890625
- keys: bfloat16 [4, 2048, 512], P('dp', 'seq'), may hold values from -0.890625 to 0.890625
- values: bfloat16 [4, 2048, 512], P('dp', 'seq'), may hold values from -6 to 6
- level_weights: float32 [4, 6, 4, 2048], P('dp', None, None, 'seq'), may hold values from 0.25 to 4
- proj: bfloat16 [512, 2048], P(None, 'seq'), may hold values from -0.25 to 0.25
- out_grad: bfloat16 [4, 2048, 2048], P('dp', 'seq'), may hold values from -0.59765625 to 0.59765625
Outputs:
- attended_out: bfloat16 [4, 2048, 2048], P('dp', 'seq')
- grad_queries: bfloat16 [4, 2048, 512], P('dp', 'seq')
- grad_keys: bfloat16 [4, 2048, 512], P('dp', 'seq')
- grad_values: bfloat16 [4, 2048, 512], P('dp', 'seq')
- grad_levels: float32 [4, 6, 4, 2048], P('dp', None, None, 'seq')
- grad_proj: float32 [512, 2048], P(None, 'seq')
All inputs are finite; a program needn't handle non-finite values.
Results may differ from a plain program's by a relative error of at most 0.0064.
Values may be sent and summed in bfloat16 or wider, within the bound.
No kernel may reach another device: no remote copies, remote signals or barrier semaphores. Data moves between devices by JAX's collectives and lax.ppermute only.
A program may use at most 64 MiB of HBM per device.

v0:
```python
import jax
import jax.numpy as jnp
from jax import lax
from jax.sharding import PartitionSpec as P


def partner_2(value, axis, stride):
    mask = 2**stride
    pairs = [(source, source ^ mask) for source in range(lax.axis_size(axis))]
    return lax.ppermute(value, axis, pairs)


def level_table(length, stretch, local_bits):
    place = lax.iota(jnp.int32, length)
    blocks = place // stretch
    apart = jnp.bitwise_xor(blocks[:, None], blocks[None, :])
    table = jnp.zeros((length, length), jnp.int32)
    for bit in range(local_bits):
        table = table + (apart >= 1 << bit).astype(jnp.int32)
    causal = place[:, None] >= place[None, :]
    return (table, causal)


def local_weights(lam, table, causal, local_bits):
    weights = jnp.zeros((lam.shape[1], table.shape[0], table.shape[1]), jnp.float32)
    for level in range(local_bits + 1):
        weights = weights + jnp.where(table[None] == level, lam[level][:, :, None], jnp.float32(0))
    return jnp.where(causal[None], weights, jnp.float32(0))


def marked_bit(index, bit):
    return jnp.bitwise_and(jnp.right_shift(index, bit), 1).astype(jnp.float32)


def shards(queries, keys, values, level_weights, proj, out_grad):
    tokens_here = queries.shape[1]
    heads = level_weights.shape[2]
    levels = level_weights.shape[1]
    width = queries.shape[2]
    size = width // heads
    scale = size ** (-0.5)
    span_count = lax.axis_size("seq")
    dev_bits = span_count.bit_length() - 1
    local_bits = levels - 1 - dev_bits
    stretch = tokens_here >> local_bits
    index = lax.axis_index("seq")
    shape = (tokens_here, heads, size)
    query = queries[0].reshape(shape)
    key = keys[0].reshape(shape)
    value = values[0].reshape(shape)
    lam = level_weights[0]
    grad_out = out_grad[0]
    table, causal = level_table(tokens_here, stretch, local_bits)
    scores = jnp.einsum("thd,shd->hts", query, key, preferred_element_type=jnp.float32)
    weights = local_weights(lam, table, causal, local_bits)
    probs = (scale * weights * scores).astype(jnp.bfloat16)
    total = jnp.einsum("hts,shd->thd", probs, value, preferred_element_type=jnp.float32)
    totals = jnp.einsum("shi,shj->hij", key, value, preferred_element_type=jnp.float32)
    running = totals
    states = []
    for bit in range(dev_bits):
        partner = partner_2(running, "seq", bit)
        states.append((marked_bit(index, bit) * partner).astype(jnp.bfloat16))
        running = running + partner
    cross = jnp.zeros_like(total)
    mapped = []
    for bit in range(dev_bits):
        image = jnp.einsum("thi,hij->thj", query, states[bit], preferred_element_type=jnp.float32)
        mapped.append(image)
        cross = cross + lam[local_bits + 1 + bit].T[:, :, None] * image
    attended = (total + scale * cross).astype(jnp.bfloat16).reshape(tokens_here, width)
    full_proj = lax.all_gather(proj, "seq", axis=1, tiled=True)
    out = jnp.dot(attended, full_proj, preferred_element_type=jnp.float32).astype(jnp.bfloat16)
    grad_att = lax.dot_general(
        grad_out, full_proj, (((1,), (1,)), ((), ())), preferred_element_type=jnp.float32
    ).astype(jnp.bfloat16)
    grad_heads = grad_att.reshape(shape)
    dprob = jnp.einsum("thd,shd->hts", grad_heads, value, preferred_element_type=jnp.float32)
    product = jnp.where(causal[None], scale * scores * dprob, jnp.float32(0))
    grads = [
        jnp.sum(jnp.where(table[None] == level, product, jnp.float32(0)), axis=2)
        for level in range(local_bits + 1)
    ]
    dscore = (scale * weights * dprob).astype(jnp.bfloat16)
    grad_q = jnp.einsum("hts,shd->thd", dscore, key, preferred_element_type=jnp.float32)
    grad_k = jnp.einsum("hts,thd->shd", dscore, query, preferred_element_type=jnp.float32)
    grad_v = jnp.einsum("hts,thd->shd", probs, grad_heads, preferred_element_type=jnp.float32)
    updates = []
    for bit in range(dev_bits):
        grads.append(scale * jnp.sum(grad_heads.astype(jnp.float32) * mapped[bit], axis=2).T)
        weighted = (
            scale * lam[local_bits + 1 + bit].T[:, :, None] * grad_heads.astype(jnp.float32)
        ).astype(jnp.bfloat16)
        updates.append(
            jnp.einsum("thi,thj->hij", query, weighted, preferred_element_type=jnp.float32)
        )
        grad_q = grad_q + jnp.einsum(
            "thj,hij->thi", weighted, states[bit], preferred_element_type=jnp.float32
        )
    pending = [marked_bit(index, bit) * updates[bit] for bit in range(dev_bits)]
    carried = jnp.zeros_like(totals)
    for bit in range(dev_bits):
        sending = jnp.stack(pending[bit:])
        arrived = partner_2(sending, "seq", bit)
        carried = carried + (1.0 - marked_bit(index, bit)) * arrived[0]
        for later in range(bit + 1, dev_bits):
            pending[later] = pending[later] + arrived[later - bit]
    returned = carried.astype(jnp.bfloat16)
    grad_k = grad_k + jnp.einsum(
        "shj,hij->shi", value, returned, preferred_element_type=jnp.float32
    )
    grad_v = grad_v + jnp.einsum("shi,hij->shj", key, returned, preferred_element_type=jnp.float32)
    shard = lax.psum_scatter(
        lax.dot_general(
            grad_out, attended, (((0,), (0,)), ((), ())), preferred_element_type=jnp.float32
        ),
        "seq",
        scatter_dimension=0,
        tiled=True,
    )
    shard = lax.psum(shard, "dp")
    grad_levels = jnp.stack(grads)[None]
    return (
        out[None],
        grad_q.astype(jnp.bfloat16).reshape(1, tokens_here, width),
        grad_k.astype(jnp.bfloat16).reshape(1, tokens_here, width),
        grad_v.astype(jnp.bfloat16).reshape(1, tokens_here, width),
        grad_levels,
        shard.T,
    )


def solution(mesh):
    return jax.shard_map(
        shards,
        mesh=mesh,
        in_specs=(
            P("dp", "seq", None),
            P("dp", "seq", None),
            P("dp", "seq", None),
            P("dp", None, None, "seq"),
            P(None, "seq"),
            P("dp", "seq", None),
        ),
        out_specs=(
            P("dp", "seq", None),
            P("dp", "seq", None),
            P("dp", "seq", None),
            P("dp", "seq", None),
            P("dp", None, None, "seq"),
            P(None, "seq"),
        ),
        check_vma=False,
    )
```

profile of v0, /device:TPU:0, one launch (start us, length us, event | category | flops | bytes accessed | tf_op | source)
XLA Modules:
  0.0 157.5 jit_solution(11511535724584984246)
XLA Ops:
  8.0 1.0 reshape_squeeze.10
  9.2 1.1 reshape_squeeze.11
  11.8 0.9 fusion.29
  12.7 1.3 fusion.31
  14.0 2.6 %collective-permute-start.1 = (f32[4,128,128]{2,1,0:T(8,128)S(1)}, f32[4,128,128]{2,1,0:T(8,128)S(1)}, u32[]{:S(2)}, u32[]{:S(2)}) collective-permute-start(f32[4,128,128]{2,1,0:T(8,128)S(1)} %add.93), channel_id=1, source_target_pairs={{0,2},{1,3},{2,0},{3,1},{4,6},{5,7},{6,4},{7,5},{8,10},{9,11},{10,... | collective-permute-start | bytes 786440 | tf_op jit(solution)/shard_map/ppermute | solution.py:10
  17.4 8.0 %collective-permute-done.1 = f32[4,128,128]{2,1,0:T(8,128)S(1)} collective-permute-done((f32[4,128,128]{2,1,0:T(8,128)S(1)}, f32[4,128,128]{2,1,0:T(8,128)S(1)}, u32[]{:S(2)}, u32[]{:S(2)}) %collective-permute-start.1) | collective-permute-done | bytes 262176 | tf_op jit(solution)/shard_map/ppermute | solution.py:10
  26.1 1.4 collective-permute-start.2
  27.5 1.1 convolution_bitcast_fusion.9
  28.6 14.4 %all-gather.2.cloned.1.call-done = bf16[512,2048]{1,0:T(8,128)(2,1)} async-done(((bf16[512,256]{1,0:T(8,128)(2,1)}), bf16[512,2048]{1,0:T(8,128)(2,1)}) %all-gather.2.cloned.1.call-update) | async-done | bytes 2097168 | tf_op jit(solution)/shard_map/all_gather | solution.py:72
  42.9 3.0 %convolution_convert_fusion.1 = bf16[256,512]{1,0:T(8,128)(2,1)} fusion(bf16[512,2048]{1,0:T(8,128)(2,1)} %all-gather.2.cloned.1.call-done, bf16[1,256,2048]{2,1,0:T(8,128)(2,1)S(1)} %copy-done), kind=kOutput, calls=%fused_computation.21 | convolution fusion | flops 537001984 | bytes 3407872 | tf_op jit(solution)/shard_map/dot_general | solution.py:74
  46.0 1.1 copy.24
  47.2 1.5 fusion.18
  49.4 2.7 %convolution_bitcast_fusion = f32[2048,512]{0,1:T(8,128)} fusion(bf16[256,512]{0,1:T(8,128)(2,1)S(1)} %bitcast.163, bf16[1,256,2048]{2,1,0:T(8,128)(2,1)S(1)} %copy-done), kind=kOutput, calls=%fused_computation | convolution fusion | flops 536870912 | bytes 5505024 | tf_op jit(solution)/shard_map/dot_general | solution.py:114
  56.5 1.5 fusion.55
  58.1 1.5 collective-permute-start.4
  60.1 12.2 %collective-permute-done.4 = f32[2,4,128,128]{2,3,1,0:T(8,128)S(1)} collective-permute-done((f32[2,4,128,128]{2,3,1,0:T(8,128)S(1)}, f32[2,4,128,128]{2,3,1,0:T(8,128)S(1)}, u32[]{:S(2)}, u32[]{:S(2)}) %collective-permute-start.4) | collective-permute-done | bytes 524320 | tf_op jit(solution)/shard_map/ppermute | solution.py:10
  73.1 1.1 collective-permute-start.5
  75.7 3.3 %fusion = bf16[1,256,2048]{2,1,0:T(8,128)(2,1)} fusion(bf16[256,512]{0,1:T(8,128)(2,1)S(1)} %bitcast.164, bf16[512,2048]{1,0:T(8,128)(2,1)} %all-gather.2.cloned.1.call-done), kind=kOutput, calls=%fused_computation.2 | convolution fusion | flops 537395200 | bytes 3407872 | tf_op jit(solution)/shard_map/dot_general | solution.py:73
  79.1 29.1 %reduce-scatter.2.cloned.1.call-done = f32[256,512]{0,1:T(8,128)} async-done(((f32[2048,512]{0,1:T(8,128)}), f32[256,512]{0,1:T(8,128)}) %reduce-scatter.2.cloned.1.call-update) | async-done | bytes 524304 | tf_op jit(solution)/shard_map/reduce_scatter | solution.py:113
  108.2 1.1 fusion.45
  109.6 0.8 copy.42
  110.6 0.8 copy.43
  111.5 37.6 %all-reduce.2.cloned.1.call-done = f32[512,256]{1,0:T(8,128)} async-done(((f32[512,256]{1,0:T(8,128)}), f32[512,256]{1,0:T(8,128)}) %all-reduce.2.cloned.1.call-update) | async-done | bytes 524304 | tf_op jit(solution)/shard_map/psum | solution.py:121
  149.1 1.9 %copy.96 = f32[512,256]{1,0:T(8,128)} copy(f32[512,256]{1,0:T(8,128)} %all-reduce.2.cloned.1.call-done) | data formatting | bytes 1048576
  (103 shorter events, 12.4 us)
Async XLA Ops:
  7.2 35.8 %copy-start = (bf16[1,256,2048]{2,1,0:T(8,128)(2,1)S(1)}, bf16[1,256,2048]{2,1,0:T(8,128)(2,1)}, u32[]{:S(2)}) copy-start(bf16[1,256,2048]{2,1,0:T(8,128)(2,1)} %param.11) | copy-start | bytes 3145732
  7.2 3.9 %copy-start.12 = (bf16[1,256,512]{2,1,0:T(8,128)(2,1)S(1)}, bf16[1,256,512]{2,1,0:T(8,128)(2,1)}, u32[]{:S(2)}) copy-start(bf16[1,256,512]{2,1,0:T(8,128)(2,1)} %param.6) | copy-start | bytes 786436
  7.2 4.0 %copy-start.19 = (f32[1,6,4,256]{3,2,1,0:T(4,128)S(1)}, f32[1,6,4,256]{3,2,1,0:T(4,128)}, u32[]{:S(2)}) copy-start(f32[1,6,4,256]{3,2,1,0:T(4,128)} %param.9) | copy-start | bytes 73732
  7.2 35.7 %all-gather.2.cloned.1.call-start = ((), (), s32[]{:S(2)}) async-start(), calls=%async_computation.1 | async-start | bytes 2359296 | tf_op jit(solution)/shard_map/all_gather | solution.py:72
  7.9 100.2 %reduce-scatter.2.cloned.1.call-start = ((), (), s32[]{:S(2)}) async-start(), calls=%async_computation.2 | async-start | bytes 4718592 | tf_op jit(solution)/shard_map/reduce_scatter | solution.py:113
  10.5 3.4 %collective-permute-start = (f32[4,128,128]{2,1,0:T(8,128)S(1)}, f32[4,128,128]{2,1,0:T(8,128)S(1)}, u32[]{:S(2)}, u32[]{:S(2)}) collective-permute-start(f32[4,128,128]{2,1,0:T(8,128)S(1)} %fusion.43), channel_id=1, source_target_pairs={{0,1},{1,0},{2,3},{3,2},{4,5},{5,4},{6,7},{7,6},{8,9},{9,8},{10,11... | collective-permute-start | bytes 786440 | tf_op jit(solution)/shard_map/ppermute | solution.py:10
  14.0 11.4 %collective-permute-start.1 = (f32[4,128,128]{2,1,0:T(8,128)S(1)}, f32[4,128,128]{2,1,0:T(8,128)S(1)}, u32[]{:S(2)}, u32[]{:S(2)}) collective-permute-start(f32[4,128,128]{2,1,0:T(8,128)S(1)} %add.93), channel_id=1, source_target_pairs={{0,2},{1,3},{2,0},{3,1},{4,6},{5,7},{6,4},{7,5},{8,10},{9,11},{10,... | collective-permute-start | bytes 786440 | tf_op jit(solution)/shard_map/ppermute | solution.py:10
  26.1 21.0 %collective-permute-start.2 = (f32[4,128,128]{2,1,0:T(8,128)}, f32[4,128,128]{2,1,0:T(8,128)S(1)}, u32[]{:S(2)}, u32[]{:S(2)}) collective-permute-start(f32[4,128,128]{2,1,0:T(8,128)} %add.95), channel_id=1, source_target_pairs={{0,4},{1,5},{2,6},{3,7},{4,0},{5,1},{6,2},{7,3},{8,12},{9,13},{10,... | collective-permute-start | bytes 786440 | tf_op jit(solution)/shard_map/ppermute | solution.py:10
  47.1 1.6 %copy-start.1 = (f32[256,4,128]{0,2,1:T(8,128)S(1)}, f32[256,4,128]{0,2,1:T(8,128)}, u32[]{:S(2)}) copy-start(f32[256,4,128]{0,2,1:T(8,128)} %convolution_bitcast_fusion.9) | copy-start | bytes 1572868
  47.1 1.6 %copy-start.5 = (f32[4,256,256]{1,2,0:T(8,128)S(1)}, f32[4,256,256]{1,2,0:T(8,128)}, u32[]{:S(2)}) copy-start(f32[4,256,256]{1,2,0:T(8,128)} %fusion.31) | copy-start | bytes 3145732
  47.1 1.6 %copy-start.13 = (pred[256,256]{0,1:T(8,128)(4,1)S(1)}, pred[256,256]{0,1:T(8,128)(4,1)}, u32[]{:S(2)}) copy-start(pred[256,256]{0,1:T(8,128)(4,1)} %get-tuple-element.31) | copy-start | bytes 196612
  47.1 1.6 %copy-start.16 = (pred[256,256]{0,1:T(8,128)(4,1)S(1)}, pred[256,256]{0,1:T(8,128)(4,1)}, u32[]{:S(2)}) copy-start(pred[256,256]{0,1:T(8,128)(4,1)} %iota_compare_fusion) | copy-start | bytes 196612
  47.1 1.6 %copy-start.21 = (f32[4,256]{1,0:T(4,128)S(1)}, f32[4,256]{1,0:T(4,128)}, u32[]{:S(2)}) copy-start(f32[4,256]{1,0:T(4,128)} %get-tuple-element.25) | copy-start | bytes 12292
  47.1 1.6 %copy-start.23 = (f32[4,256]{1,0:T(4,128)S(1)}, f32[4,256]{1,0:T(4,128)}, u32[]{:S(2)}) copy-start(f32[4,256]{1,0:T(4,128)} %get-tuple-element.26) | copy-start | bytes 12292
  47.1 1.6 %copy-start.25 = (f32[256,4]{0,1:T(4,128)S(1)}, f32[256,4]{0,1:T(4,128)}, u32[]{:S(2)}) copy-start(f32[256,4]{0,1:T(4,128)} %get-tuple-element.24) | copy-start | bytes 12292
  52.1 1.8 %copy-start.14 = (pred[256,256]{0,1:T(8,128)(4,1)S(1)}, pred[256,256]{0,1:T(8,128)(4,1)}, u32[]{:S(2)}) copy-start(pred[256,256]{0,1:T(8,128)(4,1)} %get-tuple-element.31) | copy-start | bytes 196612
  52.1 1.8 %copy-start.17 = (pred[256,256]{0,1:T(8,128)(4,1)S(1)}, pred[256,256]{0,1:T(8,128)(4,1)}, u32[]{:S(2)}) copy-start(pred[256,256]{0,1:T(8,128)(4,1)} %iota_compare_fusion) | copy-start | bytes 196612
  52.1 96.9 %all-reduce.2.cloned.1.call-start = ((), (), s32[]{:S(2)}) async-start(), calls=%async_computation.3 | async-start | bytes 1048576 | tf_op jit(solution)/shard_map/psum | solution.py:121
  53.6 4.4 %collective-permute-start.3 = (f32[3,4,128,128]{2,3,1,0:T(8,128)S(1)}, f32[3,4,128,128]{2,3,1,0:T(8,128)S(1)}, u32[]{:S(2)}, u32[]{:S(2)}) collective-permute-start(f32[3,4,128,128]{2,3,1,0:T(8,128)S(1)} %pad_maximum_fusion), channel_id=1, source_target_pairs={{0,1},{1,0},{2,3},{3,2},{4,5},{5,4},{6,7},{7,6},{8,9},{9,8},{10,11... | collective-permute-start | bytes 2359304 | tf_op jit(solution)/shard_map/ppermute | solution.py:10
  58.0 14.2 %copy-start.2 = (f32[3,4,128,128]{2,3,1,0:T(8,128)}, f32[3,4,128,128]{2,3,1,0:T(8,128)S(1)}, u32[]{:S(2)}) copy-start(f32[3,4,128,128]{2,3,1,0:T(8,128)S(1)} %collective-permute-done.3) | copy-start | bytes 2359300
  58.1 14.1 %collective-permute-start.4 = (f32[2,4,128,128]{2,3,1,0:T(8,128)S(1)}, f32[2,4,128,128]{2,3,1,0:T(8,128)S(1)}, u32[]{:S(2)}, u32[]{:S(2)}) collective-permute-start(f32[2,4,128,128]{2,3,1,0:T(8,128)S(1)} %pad_maximum_fusion.1), channel_id=1, source_target_pairs={{0,2},{1,3},{2,0},{3,1},{4,6},{5,7},{6,4},{7,5},{8,10},{9,11},{10,... | collective-permute-start | bytes 1572872 | tf_op jit(solution)/shard_map/ppermute | solution.py:10
  73.1 35.0 %collective-permute-start.5 = (f32[1,4,128,128]{2,3,1,0:T(8,128)}, f32[1,4,128,128]{2,3,1,0:T(8,128)}, u32[]{:S(2)}, u32[]{:S(2)}) collective-permute-start(f32[1,4,128,128]{2,3,1,0:T(8,128)} %fusion.20), channel_id=1, source_target_pairs={{0,4},{1,5},{2,6},{3,7},{4,0},{5,1},{6,2},{7,3},{8,12},{9,13},{10,... | collective-permute-start | bytes 786440 | tf_op jit(solution)/shard_map/ppermute | solution.py:10
  75.7 32.5 %copy-start.11 = (f32[2,4,128,128]{2,3,1,0:T(8,128)S(1)}, f32[2,4,128,128]{2,3,1,0:T(8,128)}, u32[]{:S(2)}) copy-start(f32[2,4,128,128]{2,3,1,0:T(8,128)} %copy-done.10) | copy-start | bytes 1572868
  79.1 31.3 %copy-start.9 = (f32[4,128,256]{2,1,0:T(8,128)S(1)}, f32[4,128,256]{2,1,0:T(8,128)}, u32[]{:S(2)}) copy-start(f32[4,128,256]{2,1,0:T(8,128)} %fusion.55) | copy-start | bytes 1572868
  (14 other events, 16.6 us)
Sparse Core Ops, SparseCore 0:
  9.9 32.9 all-gather.1
  52.2 55.8 reduce-scatter.1
  110.5 38.5 all-reduce.1
where the time goes:
time: 158 us; the launch traced here: 157 us
  waiting for transfers between devices  102 us (65%)
  matrix products  19.2 us (12%)
  between operations  14.2 us (9%)
  local copies, waits for them, and re-layouts  10.2 us (6%)
  starting transfers between devices  7.56 us (5%)
  other arithmetic  4.34 us (3%)
    psum x1, waiting for transfers between devices, shards(): shard = lax.psum(shard, 'dp')  37.6 us
    reduce_scatter x1, waiting for transfers between devices, shards(): lax.psum_scatter(lax.dot_general(grad_out, attended, (((0,), (0,)), ((),...  29.1 us
    ppermute x6, waiting for transfers between devices, partner_2(): return lax.ppermute(value, axis, pairs)  20.1 us
    all_gather x1, waiting for transfers between devices, shards(): full_proj = lax.all_gather(proj, 'seq', axis=1, tiled=True)  14.4 us
    ppermute x6, starting transfers between devices, partner_2(): return lax.ppermute(value, axis, pairs)  7.44 us
    unnamed x65, local copies, waits for them, and re-layouts  6.16 us
    dot_general x1, matrix products, shards(): jnp.dot(attended, full_proj, preferred_element_type=jnp.float32)  3.35 us
  transfers between devices with their start and end apart: 9, of which 5 were waited for; matrix products, arithmetic and copies ran while one was open for 16% of the time, Pallas kernels for 0%

commit v1 on v0

--- a/solution.py
+++ b/solution.py
@@ -118,7 +118,7 @@
         scatter_dimension=0,
         tiled=True,
     )
-    shard = lax.psum(shard, "dp")
+    shard = jnp.sum(lax.all_gather(shard, "dp"), axis=0)
     grad_levels = jnp.stack(grads)[None]
     return (
         out[None],

time: 158 us -> 163 us (1.032)
  other arithmetic: 4.34 us -> 9.97 us
  waiting for transfers between devices: 102 us -> 97.1 us
  matrix products: 19.2 us -> 23.6 us
    psum x1 -> x0, waiting for transfers between devices: 37.6 us -> none  [shards(): shard = lax.psum(shard, 'dp')]
    reduce_scatter x1, waiting for transfers between devices: 29.1 us -> 45.5 us  [shards(): lax.psum_scatter(lax.dot_general(grad_out, attended, (((0,), (0,)), ((),...]
    all_gather x0 -> x1, waiting for transfers between devices: none -> 15.9 us  [shards(): shard = jnp.sum(lax.all_gather(shard, 'dp'), axis=0)]
    another operation x4, other arithmetic: 0.96 us -> 3.95 us  [shards(): sending = jnp.stack(pending[bit:])]
    unnamed x65 -> x74, local copies, waits for them, and re-layouts: 6.16 us -> 3.35 us
    all_gather x0 -> x1, local copies, waits for them, and re-layouts: none -> 2.2 us  [shards(): shard = jnp.sum(lax.all_gather(shard, 'dp'), axis=0)]
    reduce_sum x0 -> x1, other arithmetic: none -> 2.14 us  [shards(): shard = jnp.sum(lax.all_gather(shard, 'dp'), axis=0)]
    dot_general x1, matrix products: 0.64 us -> 2.75 us  [shards(): jnp.einsum('hts,thd->shd', dscore, query, preferred_element_type=jnp.floa...]
  transfers between devices with their start and end apart: 9 -> 9, of which waited for: 5 -> 6; matrix products, arithmetic and copies ran while one was open for 16% -> 20% of each run, Pallas kernels for 0% -> 0%
where the time goes in v1:
time: 163 us; the launch traced here: 162 us
  waiting for transfers between devices  97.1 us (60%)
  matrix products  23.6 us (14%)
  between operations  14.2 us (9%)
  other arithmetic  9.97 us (6%)
  local copies, waits for them, and re-layouts  9.61 us (6%)
  starting transfers between devices  7.91 us (5%)
    reduce_scatter x1, waiting for transfers between devices, shards(): lax.psum_scatter(lax.dot_general(grad_out, attended, (((0,), (0,)), ((),...  45.5 us
    ppermute x6, waiting for transfers between devices, partner_2(): return lax.ppermute(value, axis, pairs)  20.6 us
    all_gather x1, waiting for transfers between devices, shards(): shard = jnp.sum(lax.all_gather(shard, 'dp'), axis=0)  15.9 us
    all_gather x1, waiting for transfers between devices, shards(): full_proj = lax.all_gather(proj, 'seq', axis=1, tiled=True)  14.4 us
    ppermute x6, starting transfers between devices, partner_2(): return lax.ppermute(value, axis, pairs)  7.8 us
    another operation x4, other arithmetic, shards(): sending = jnp.stack(pending[bit:])  3.95 us
    dot_general x3, matrix products, shards(): jnp.einsum('thi,hij->thj', query, states[bit], preferred_element_type=jnp...  3.41 us
    dot_general x1, matrix products, shards(): jnp.dot(attended, full_proj, preferred_element_type=jnp.float32)  3.36 us
  transfers between devices with their start and end apart: 9, of which 6 were waited for; matrix products, arithmetic and copies ran while one was open for 20% of the time, Pallas kernels for 0%

profile of v1, /device:TPU:0, one launch (start us, length us, event | category | flops | bytes accessed | tf_op | source)
XLA Modules:
  0.0 162.4 jit_solution(8227577753078349684)
XLA Ops:
  9.2 1.1 reshape_squeeze.11
  12.6 1.3 fusion.31
  13.9 2.6 %collective-permute-start.1 = (f32[4,128,128]{2,1,0:T(8,128)S(1)}, f32[4,128,128]{2,1,0:T(8,128)S(1)}, u32[]{:S(2)}, u32[]{:S(2)}) collective-permute-start(f32[4,128,128]{2,1,0:T(8,128)S(1)} %add.91), channel_id=1, source_target_pairs={{0,2},{1,3},{2,0},{3,1},{4,6},{5,7},{6,4},{7,5},{8,10},{9,11},{10,... | collective-permute-start | bytes 786440 | tf_op jit(solution)/shard_map/ppermute | solution.py:10
  17.4 8.0 %collective-permute-done.1 = f32[4,128,128]{2,1,0:T(8,128)S(1)} collective-permute-done((f32[4,128,128]{2,1,0:T(8,128)S(1)}, f32[4,128,128]{2,1,0:T(8,128)S(1)}, u32[]{:S(2)}, u32[]{:S(2)}) %collective-permute-start.1) | collective-permute-done | bytes 262176 | tf_op jit(solution)/shard_map/ppermute | solution.py:10
  26.1 1.4 collective-permute-start.2
  28.5 14.4 %all-gather.4.cloned.1.call-done = bf16[512,2048]{1,0:T(8,128)(2,1)} async-done(((bf16[512,256]{1,0:T(8,128)(2,1)}), bf16[512,2048]{1,0:T(8,128)(2,1)}) %all-gather.4.cloned.1.call-update) | async-done | bytes 2097168 | tf_op jit(solution)/shard_map/all_gather | solution.py:72
  42.9 3.0 %convolution_convert_fusion.1 = bf16[256,512]{1,0:T(8,128)(2,1)} fusion(bf16[512,2048]{1,0:T(8,128)(2,1)} %all-gather.4.cloned.1.call-done, bf16[1,256,2048]{2,1,0:T(8,128)(2,1)S(1)} %copy-done), kind=kOutput, calls=%fused_computation.21 | convolution fusion | flops 537001984 | bytes 3407872 | tf_op jit(solution)/shard_map/dot_general | solution.py:74
  47.2 2.1 %fusion.18 = (f32[256,4]{0,1:T(4,128)S(1)}, f32[256,4]{0,1:T(4,128)S(1)}, f32[256,4]{0,1:T(4,128)}, f32[256,4,128]{0,2,1:T(8,128)S(1)}) fusion(bf16[256,512]{0,1:T(8,128)(2,1)S(1)} %copy.24, f32[256,4,128]{0,2,1:T(8,128)} %convolution_bitcast_fusion.9, f32[256,4,128]{0,2,1:T(8,128)S(1)} %convolution_bitcast_fusion.10, ...), kind=kOutput, calls=%fused_computation.49 | convolution fusion | flops 34599936 | bytes 2371588 | tf_op jit(solution)/shard_map/thi,hij->thj/dot_general | solution.py:68
  50.0 2.7 %convolution_bitcast_fusion = f32[2048,512]{0,1:T(8,128)} fusion(bf16[256,512]{0,1:T(8,128)(2,1)S(1)} %bitcast.165, bf16[1,256,2048]{2,1,0:T(8,128)(2,1)S(1)} %copy-done), kind=kOutput, calls=%fused_computation | convolution fusion | flops 536870912 | bytes 5505024 | tf_op jit(solution)/shard_map/dot_general | solution.py:114
  56.2 1.1 convolution_bitcast_fusion.5
  57.3 1.4 convolution_bitcast_fusion.1
  58.7 45.5 %reduce-scatter.2.cloned.1.call-done = f32[256,512]{0,1:T(8,128)} async-done(((f32[2048,512]{0,1:T(8,128)}), f32[256,512]{0,1:T(8,128)}) %reduce-scatter.2.cloned.1.call-update) | async-done | bytes 524304 | tf_op jit(solution)/shard_map/reduce_scatter | solution.py:113
  104.3 2.8 %convolution_bitcast_fusion.4 = f32[256,4,128]{0,2,1:T(8,128)} fusion(bf16[256,4,128]{2,1,0:T(4,128)(2,1)S(1)} %reshape_squeeze.9, f32[4,256,256]{1,2,0:T(8,128)} %copy-done.33, f32[4,256]{1,0:T(4,128)S(1)} %copy-done.26, f32[4,256]{1,0:T(4,128)S(1)} %copy-done.28, f32[4,256]{1,0:T(4,128)S(1)} %copy-done.24, pred[256,256]{0,1:T(8,128)(4,1)S(1)} %copy-done.17, ...), kind=kOutput, calls=%fused_computation.6 | convolution fusion | flops 69468160 | bytes 2109440 | tf_op jit(solution)/shard_map/hts,thd->shd/dot_general | solution.py:86
  107.0 1.4 fusion.55
  108.5 1.2 fusion.26
  109.7 1.5 collective-permute-start.4
  111.8 11.5 %collective-permute-done.4 = f32[2,4,128,128]{2,3,1,0:T(8,128)S(1)} collective-permute-done((f32[2,4,128,128]{2,3,1,0:T(8,128)S(1)}, f32[2,4,128,128]{2,3,1,0:T(8,128)S(1)}, u32[]{:S(2)}, u32[]{:S(2)}) %collective-permute-start.4) | collective-permute-done | bytes 524320 | tf_op jit(solution)/shard_map/ppermute | solution.py:10
  123.3 1.7 %fusion.20 = f32[1,4,128,128]{2,3,1,0:T(8,128)} fusion(f32[2,4,128,128]{2,3,1,0:T(8,128)S(1)} %collective-permute-done.4, f32[3,4,128,128]{2,3,1,0:T(8,128)} %collective-permute-done.3, f32[4,128,128]{2,1,0:T(8,128)S(1)} %convolution_multiply_fusion), kind=kLoop, calls=%fused_computation.55 | loop fusion | flops 131072 | bytes 1048576 | tf_op jit(solution)/shard_map/stack | solution.py:103
  125.0 1.5 collective-permute-start.5
  127.9 3.4 %fusion = bf16[1,256,2048]{2,1,0:T(8,128)(2,1)} fusion(bf16[256,512]{0,1:T(8,128)(2,1)S(1)} %bitcast.166, bf16[512,2048]{1,0:T(8,128)(2,1)} %all-gather.4.cloned.1.call-done), kind=kOutput, calls=%fused_computation.2 | convolution fusion | flops 537395200 | bytes 3407872 | tf_op jit(solution)/shard_map/dot_general | solution.py:73
  131.3 1.1 collective-permute-done.5
  135.6 15.9 %all-gather.6.cloned.1.call-done = f32[1024,512]{0,1:T(8,128)} async-done(((f32[256,512]{0,1:T(8,128)}), f32[1024,512]{0,1:T(8,128)}) %all-gather.6.cloned.1.call-update) | async-done | bytes 2097168 | tf_op jit(solution)/shard_map/all_gather | solution.py:121
  151.5 2.2 %reshape.193 = f32[4,256,512]{1,0,2:T(4,128)S(1)} reshape(f32[1024,512]{0,1:T(8,128)} %all-gather.6.cloned.1.call-done) | data formatting | bytes 4194304 | tf_op jit(solution)/shard_map/all_gather | solution.py:121
  153.7 2.1 %reduce_sum.69 = f32[256,512]{0,1:T(8,128)} reduce(f32[4,256,512]{1,0,2:T(4,128)S(1)} %reshape.193, f32[]{:T(128)} %constant.38.clone.1), dimensions={0}, to_apply=%region_7.8 | reduce | flops 393216 | bytes 2621444 | tf_op jit(solution)/shard_map/reduce_sum | solution.py:121
  (114 shorter events, 17.4 us)
Async XLA Ops:
  7.2 35.8 %copy-start = (bf16[1,256,2048]{2,1,0:T(8,128)(2,1)S(1)}, bf16[1,256,2048]{2,1,0:T(8,128)(2,1)}, u32[]{:S(2)}) copy-start(bf16[1,256,2048]{2,1,0:T(8,128)(2,1)} %param.11) | copy-start | bytes 3145732
  7.2 3.9 %copy-start.15 = (bf16[1,256,512]{2,1,0:T(8,128)(2,1)S(1)}, bf16[1,256,512]{2,1,0:T(8,128)(2,1)}, u32[]{:S(2)}) copy-start(bf16[1,256,512]{2,1,0:T(8,128)(2,1)} %param.6) | copy-start | bytes 786436
  7.2 4.0 %copy-start.20 = (f32[1,6,4,256]{3,2,1,0:T(4,128)S(1)}, f32[1,6,4,256]{3,2,1,0:T(4,128)}, u32[]{:S(2)}) copy-start(f32[1,6,4,256]{3,2,1,0:T(4,128)} %param.9) | copy-start | bytes 73732
  7.2 35.7 %all-gather.4.cloned.1.call-start = ((), (), s32[]{:S(2)}) async-start(), calls=%async_computation.1 | async-start | bytes 2359296 | tf_op jit(solution)/shard_map/all_gather | solution.py:72
  7.9 96.3 %reduce-scatter.2.cloned.1.call-start = ((), (), s32[]{:S(2)}) async-start(), calls=%async_computation.2 | async-start | bytes 4718592 | tf_op jit(solution)/shard_map/reduce_scatter | solution.py:113
  10.5 3.4 %collective-permute-start = (f32[4,128,128]{2,1,0:T(8,128)S(1)}, f32[4,128,128]{2,1,0:T(8,128)S(1)}, u32[]{:S(2)}, u32[]{:S(2)}) collective-permute-start(f32[4,128,128]{2,1,0:T(8,128)S(1)} %fusion.43), channel_id=1, source_target_pairs={{0,1},{1,0},{2,3},{3,2},{4,5},{5,4},{6,7},{7,6},{8,9},{9,8},{10,11... | collective-permute-start | bytes 786440 | tf_op jit(solution)/shard_map/ppermute | solution.py:10
  11.8 37.4 %copy-start.23 = (f32[4,256]{1,0:T(4,128)}, f32[4,256]{1,0:T(4,128)S(1)}, u32[]{:S(2)}) copy-start(f32[4,256]{1,0:T(4,128)S(1)} %get-tuple-element.23) | copy-start | bytes 12292
  11.8 37.4 %copy-start.25 = (f32[4,256]{1,0:T(4,128)}, f32[4,256]{1,0:T(4,128)S(1)}, u32[]{:S(2)}) copy-start(f32[4,256]{1,0:T(4,128)S(1)} %get-tuple-element.25) | copy-start | bytes 12292
  13.9 11.4 %collective-permute-start.1 = (f32[4,128,128]{2,1,0:T(8,128)S(1)}, f32[4,128,128]{2,1,0:T(8,128)S(1)}, u32[]{:S(2)}, u32[]{:S(2)}) collective-permute-start(f32[4,128,128]{2,1,0:T(8,128)S(1)} %add.91), channel_id=1, source_target_pairs={{0,2},{1,3},{2,0},{3,1},{4,6},{5,7},{6,4},{7,5},{8,10},{9,11},{10,... | collective-permute-start | bytes 786440 | tf_op jit(solution)/shard_map/ppermute | solution.py:10
  26.1 21.0 %collective-permute-start.2 = (f32[4,128,128]{2,1,0:T(8,128)}, f32[4,128,128]{2,1,0:T(8,128)S(1)}, u32[]{:S(2)}, u32[]{:S(2)}) collective-permute-start(f32[4,128,128]{2,1,0:T(8,128)} %add.93), channel_id=1, source_target_pairs={{0,4},{1,5},{2,6},{3,7},{4,0},{5,1},{6,2},{7,3},{8,12},{9,13},{10,... | collective-permute-start | bytes 786440 | tf_op jit(solution)/shard_map/ppermute | solution.py:10
  50.0 2.7 %copy-start.3 = (bf16[256,4,128]{0,2,1:T(8,128)(2,1)}, bf16[256,4,128]{0,2,1:T(8,128)(2,1)S(1)}, u32[]{:S(2)}) copy-start(bf16[256,4,128]{0,2,1:T(8,128)(2,1)S(1)} %fusion.7) | copy-start | bytes 786436
  52.7 2.8 %copy-start.17 = (pred[256,256]{0,1:T(8,128)(4,1)S(1)}, pred[256,256]{0,1:T(8,128)(4,1)}, u32[]{:S(2)}) copy-start(pred[256,256]{0,1:T(8,128)(4,1)} %get-tuple-element.31) | copy-start | bytes 196612
  52.7 2.7 %copy-start.19 = (pred[256,256]{0,1:T(8,128)(4,1)S(1)}, pred[256,256]{0,1:T(8,128)(4,1)}, u32[]{:S(2)}) copy-start(pred[256,256]{0,1:T(8,128)(4,1)} %iota_compare_fusion) | copy-start | bytes 196612
  52.7 98.8 %all-gather.6.cloned.1.call-start = ((), (), s32[]{:S(2)}) async-start(), calls=%async_computation.3 | async-start | bytes 2621440 | tf_op jit(solution)/shard_map/all_gather | solution.py:121
  55.2 53.3 %collective-permute-start.3 = (f32[3,4,128,128]{2,3,1,0:T(8,128)}, f32[3,4,128,128]{2,3,1,0:T(8,128)}, u32[]{:S(2)}, u32[]{:S(2)}) collective-permute-start(f32[3,4,128,128]{2,3,1,0:T(8,128)} %pad_maximum_fusion), channel_id=1, source_target_pairs={{0,1},{1,0},{2,3},{3,2},{4,5},{5,4},{6,7},{7,6},{8,9},{9,8},{10,11... | collective-permute-start | bytes 2359304 | tf_op jit(solution)/shard_map/ppermute | solution.py:10
  104.3 2.8 %copy-start.9 = (f32[4,256,256]{1,2,0:T(8,128)S(1)}, f32[4,256,256]{1,2,0:T(8,128)}, u32[]{:S(2)}) copy-start(f32[4,256,256]{1,2,0:T(8,128)} %fusion.31) | copy-start | bytes 3145732
  104.3 4.2 %copy-start.32 = (f32[6,4,256]{2,1,0:T(4,128)}, f32[6,4,256]{2,1,0:T(4,128)S(1)}, u32[]{:S(2)}) copy-start(f32[6,4,256]{2,1,0:T(4,128)S(1)} %constant_dynamic-update-slice_fusion.1) | copy-start | bytes 73732
  108.5 3.0 %copy-start.1 = (f32[256,4,128]{0,2,1:T(8,128)S(1)}, f32[256,4,128]{0,2,1:T(8,128)}, u32[]{:S(2)}) copy-start(f32[256,4,128]{0,2,1:T(8,128)} %convolution_bitcast_fusion.5) | copy-start | bytes 1572868
  108.5 3.0 %copy-start.14 = (f32[256,4,128]{0,2,1:T(8,128)S(1)}, f32[256,4,128]{0,2,1:T(8,128)}, u32[]{:S(2)}) copy-start(f32[256,4,128]{0,2,1:T(8,128)} %convolution_bitcast_fusion.1) | copy-start | bytes 1572868
  109.7 13.6 %collective-permute-start.4 = (f32[2,4,128,128]{2,3,1,0:T(8,128)S(1)}, f32[2,4,128,128]{2,3,1,0:T(8,128)S(1)}, u32[]{:S(2)}, u32[]{:S(2)}) collective-permute-start(f32[2,4,128,128]{2,3,1,0:T(8,128)S(1)} %pad_maximum_fusion.1), channel_id=1, source_target_pairs={{0,2},{1,3},{2,0},{3,1},{4,6},{5,7},{6,4},{7,5},{8,10},{9,11},{10,... | collective-permute-start | bytes 1572872 | tf_op jit(solution)/shard_map/ppermute | solution.py:10
  111.5 16.4 %copy-start.4 = (bf16[256,4,128]{0,2,1:T(8,128)(2,1)S(1)}, bf16[256,4,128]{0,2,1:T(8,128)(2,1)}, u32[]{:S(2)}) copy-start(bf16[256,4,128]{0,2,1:T(8,128)(2,1)} %copy-done.3) | copy-start | bytes 786436
  125.0 7.4 %collective-permute-start.5 = (f32[1,4,128,128]{2,3,1,0:T(8,128)}, f32[1,4,128,128]{2,3,1,0:T(8,128)S(1)}, u32[]{:S(2)}, u32[]{:S(2)}) collective-permute-start(f32[1,4,128,128]{2,3,1,0:T(8,128)} %fusion.20), channel_id=1, source_target_pairs={{0,4},{1,5},{2,6},{3,7},{4,0},{5,1},{6,2},{7,3},{8,12},{9,13},{10,... | collective-permute-start | bytes 786440 | tf_op jit(solution)/shard_map/ppermute | solution.py:10
  127.9 5.5 %copy-start.13 = (f32[256,4,128]{0,2,1:T(8,128)S(1)}, f32[256,4,128]{0,2,1:T(8,128)}, u32[]{:S(2)}) copy-start(f32[256,4,128]{0,2,1:T(8,128)} %convolution_bitcast_fusion.4) | copy-start | bytes 1572868
  131.3 3.2 %copy-start.12 = (f32[4,128,256]{2,1,0:T(8,128)S(1)}, f32[4,128,256]{2,1,0:T(8,128)}, u32[]{:S(2)}) copy-start(f32[4,128,256]{2,1,0:T(8,128)} %fusion.55) | copy-start | bytes 1572868
  (19 other events, 37.3 us)
Sparse Core Ops, SparseCore 0:
  9.9 32.9 all-gather.3
  52.8 51.3 reduce-scatter.1
  105.8 45.6 all-gather.5
